TPU v7x, 32 devices: a whole 2x2x4 slice. The times are simulated.
32 devices in a mesh: row: 8 (over z, core), col: 4 (over y, x).
Axes of the slice: x: 2, y: 2, z: 4, core: 2. Of those that a mesh axis runs over, the one named last changes fastest.
Arguments:
- u_start: float32 [128, 131072], P('col', 'row'), may hold values from -24 to 24
- v_start: float32 [128, 65536], P('row', 'col'), may hold values from -24 to 24
- keep_u: float32 [128, 40], replicated, may hold values from -1 to 1, as said below
- keep_v: float32 [128, 40], replicated, may hold values from -1 to 1, as said below
- v_next: float32 [65536], P(('col', 'row')), may hold values from -96 to 96
- tile_blocks: bfloat16 [2048, 256, 256], P(('row', 'col')), may hold values from -0.375 to 0.375
- tile_rows: int32 [2048], P(('row', 'col')), may hold values from 0 to 63
- tile_cols: int32 [2048], P(('row', 'col')), may hold values from 0 to 63
- tile_count: int32 [32], P(('row', 'col')), may hold values from 32 to 64
Outputs:
- u_basis: float32 [42, 131072], P(None, ('row', 'col'))
- v_basis: float32 [43, 65536], P(None, ('col', 'row'))
- bidiagonal: float32 [2, 2], replicated
Inputs may be any that keep to these rules, and one draw needn't show every extreme that they name: `tile_rows`: tile row within the device's row group. `tile_cols`: tile column within the device's column group. `tile_count`: slots at this index and beyond hold no tile. `keep_u`: the columns are orthonormal. `keep_v`: the columns are orthonormal.
All inputs are finite; a program needn't handle non-finite values.
Results may differ from a plain program's by a relative error of at most 0.00155.
Values may be sent and summed in bfloat16 or wider, within the bound.
A program may use at most 64 MiB of HBM per device.

v0:
```python
import jax
import jax.numpy as jnp
from jax import lax
from jax.sharding import PartitionSpec as P

STEPS = 2
HIGH = lax.Precision.HIGHEST


def orthonormal(basis_rows, vector, length, gram_matrix):
    first_coef = lax.psum(jnp.dot(basis_rows, vector, precision=HIGH), ("row", "col")) / length
    once_clean = vector - jnp.dot(first_coef, basis_rows, precision=HIGH)
    second_coef, mean_square = lax.psum(
        (jnp.dot(basis_rows, once_clean, precision=HIGH), jnp.sum(once_clean * once_clean)),
        ("row", "col"),
    )
    second_coef = second_coef / length
    gram_coef = jnp.dot(gram_matrix, second_coef, precision=HIGH)
    mean_square = (
        mean_square / length
        - 2.0 * jnp.dot(second_coef, second_coef, precision=HIGH)
        + jnp.dot(second_coef, gram_coef, precision=HIGH)
    )
    twice_clean = once_clean - jnp.dot(second_coef, basis_rows, precision=HIGH)
    scale_now = jnp.sqrt(mean_square + 1e-06)
    cross_terms = (second_coef - gram_coef) / scale_now
    corner = mean_square / (scale_now * scale_now)
    upper_part = jnp.concatenate([gram_matrix, cross_terms[:, None]], axis=1)
    bottom = jnp.concatenate([cross_terms, corner[None]])[None, :]
    grown = jnp.concatenate([upper_part, bottom], axis=0)
    return (twice_clean / scale_now, scale_now, grown)


def per_device(
    u_start, v_start, keep_u, keep_v, v_next, tile_blocks, tile_rows, tile_cols, tile_count
):
    row_total = lax.axis_size("row")
    col_total = lax.axis_size("col")
    u_here = u_start.shape[0]
    u_part = lax.dynamic_slice_in_dim(keep_u, lax.axis_index("col") * u_here, u_here, 0)
    u_kept = lax.psum_scatter(
        jnp.dot(u_part.T, u_start, precision=HIGH), "col", scatter_dimension=1, tiled=True
    )
    v_here = v_start.shape[0]
    v_part = lax.dynamic_slice_in_dim(keep_v, lax.axis_index("row") * v_here, v_here, 0)
    v_kept = lax.psum_scatter(
        jnp.dot(v_part.T, v_start, precision=HIGH), "row", scatter_dimension=1, tiled=True
    )
    u_length = u_kept.shape[1] * row_total * col_total
    v_length = v_kept.shape[1] * row_total * col_total
    gram_left, gram_right = lax.psum(
        (jnp.dot(u_kept, u_kept.T, precision=HIGH), jnp.dot(v_kept, v_kept.T, precision=HIGH)),
        ("row", "col"),
    )
    gram_left = gram_left / u_length
    gram_right = gram_right / v_length
    tile_size = tile_blocks.shape[1]
    slot_total = tile_blocks.shape[0]
    row_blocks = u_kept.shape[1] * col_total // tile_size
    col_blocks = v_kept.shape[1] * row_total // tile_size
    active = (jnp.arange(slot_total, dtype=jnp.int32) < tile_count[0]).astype(jnp.float32)
    row_hot = (tile_rows[None, :] == jnp.arange(row_blocks, dtype=jnp.int32)[:, None]).astype(
        jnp.float32
    ) * active[None, :]
    col_hot = (tile_cols[None, :] == jnp.arange(col_blocks, dtype=jnp.int32)[:, None]).astype(
        jnp.float32
    ) * active[None, :]
    first_right, beta_start, gram_right = orthonormal(v_kept, v_next, v_length, gram_right)
    left_rows = u_kept
    right_rows = jnp.concatenate([v_kept, first_right[None, :]], axis=0)
    current = first_right
    alpha_list = []
    beta_list = []
    for iteration in range(STEPS):
        forward_gathered = lax.all_gather(current.astype(jnp.bfloat16), "row", axis=0, tiled=True)
        forward_picked = forward_gathered.reshape(col_blocks, tile_size)[tile_cols]
        forward_products = jnp.einsum(
            "tij,tj->ti", tile_blocks, forward_picked, preferred_element_type=jnp.float32
        )
        forward_partial_value = jnp.dot(row_hot, forward_products, precision=HIGH).reshape(-1)
        image = lax.psum_scatter(forward_partial_value, "col", scatter_dimension=0, tiled=True)
        left_new, alpha, gram_left = orthonormal(left_rows, image, u_length, gram_left)
        left_rows = jnp.concatenate([left_rows, left_new[None, :]], axis=0)
        gathered = lax.all_gather(left_new.astype(jnp.bfloat16), "col", axis=0, tiled=True)
        picked = gathered.reshape(row_blocks, tile_size)[tile_rows]
        products = jnp.einsum("tij,ti->tj", tile_blocks, picked, preferred_element_type=jnp.float32)
        partial_value = jnp.dot(col_hot, products, precision=HIGH).reshape(-1)
        back_image = lax.psum_scatter(partial_value, "row", scatter_dimension=0, tiled=True)
        current, beta, gram_right = orthonormal(right_rows, back_image, v_length, gram_right)
        right_rows = jnp.concatenate([right_rows, current[None, :]], axis=0)
        alpha_list.append(alpha)
        beta_list.append(beta)
    bidiagonal = jnp.stack([jnp.stack(alpha_list), jnp.stack(beta_list)])
    return (left_rows, right_rows, bidiagonal)


def solution(mesh):
    return jax.shard_map(
        per_device,
        mesh=mesh,
        in_specs=(
            P("col", "row"),
            P("row", "col"),
            P(),
            P(),
            P(("col", "row")),
            P(("row", "col"), None, None),
            P(("row", "col")),
            P(("row", "col")),
            P(("row", "col")),
        ),
        out_specs=(P(None, ("row", "col")), P(None, ("col", "row")), P()),
        check_vma=False,
    )
```

profile of v0, /device:TPU:0, one launch (start us, length us, event | category | flops | bytes accessed | tf_op | source)
XLA Modules:
  0.0 769.2 jit_solution(18316599006986476255)
XLA Ops:
  7.3 5.1 fusion.49
  12.5 4.5 fusion.51
  20.3 32.9 %reduce-scatter.5.cloned.1.call-done = f32[40,2048]{1,0:T(8,128)} async-done(((f32[40,16384]{1,0:T(8,128)}), f32[40,2048]{1,0:T(8,128)}) %reduce-scatter.5.cloned.1.call-update) | async-done | bytes 327696 | tf_op jit(solution)/shard_map/reduce_scatter | solution.py:46
  54.5 38.4 %psum.119 = f32[40]{0:T(128)S(1)} all-reduce(f32[40]{0:T(128)S(1)} %convolution_bitcast_fusion.18), channel_id=1, replica_groups=mesh['row'=8,'col'=4] {'row','col'}, use_global_device_ids=true, to_apply=%region_2.0 | all-reduce | flops 40 | bytes 320 | tf_op jit(solution)/shard_map/psum | solution.py:11
  96.0 1.6 fusion.128
  97.6 42.2 %all-reduce.8 = (f32[40]{0:T(128)S(1)}, f32[]{:T(128)}, f32[40,40]{1,0:T(8,128)S(1)}) all-reduce(f32[40]{0:T(128)S(1)} %convolution_bitcast_fusion.17, f32[]{:T(128)} %get-tuple-element.37, f32[40,40]{1,0:T(8,128)S(1)} %fusion.128), channel_id=1, replica_groups=mesh['row'=8,'col'=4] {'row','col'}, use_global_device_ids=true, to_apply=%region_3.0 | all-reduce | flops 1641 | bytes 13128 | tf_op jit(solution)/shard_map/psum | solution.py:13
  143.9 14.1 %all_gather.12 = bf16[16384]{0:T(1024)(128)(2,1)S(1)} all-gather(bf16[2048]{0:T(1024)(128)(2,1)S(1)} %get-tuple-element.35), channel_id=1, replica_groups=mesh['row'=8,'col'=4] {'row'}, dimensions={0}, use_global_device_ids=true | all-gather | bytes 36864 | tf_op jit(solution)/shard_map/all_gather | solution.py:75
  158.7 5.6 fusion.24
  165.5 1.9 fusion.129
  167.5 39.4 %all-reduce.14.cloned.1.call-done = f32[16384]{0:T(1024)} async-done(((f32[16384]{0:T(1024)}), f32[16384]{0:T(1024)}) %all-reduce.14.cloned.1.call-update) | async-done | bytes 65552
  207.6 1.7 convolution_bitcast_fusion.11
  209.3 39.4 %psum.123 = f32[40]{0:T(128)S(1)} all-reduce(f32[40]{0:T(128)S(1)} %convolution_bitcast_fusion.11), channel_id=1, replica_groups=mesh['row'=8,'col'=4] {'row','col'}, use_global_device_ids=true, to_apply=%region_8.0 | all-reduce | flops 40 | bytes 320 | tf_op jit(solution)/shard_map/psum | solution.py:11
  248.7 1.5 fusion.77
  251.5 1.7 convolution_bitcast_fusion.10
  253.2 41.4 %all-reduce.7 = (f32[40]{0:T(128)S(1)}, f32[]{:T(128)}, f32[40,40]{1,0:T(8,128)S(1)}) all-reduce(f32[40]{0:T(128)S(1)} %convolution_bitcast_fusion.10, f32[]{:T(128)} %get-tuple-element.33, f32[40,40]{1,0:T(8,128)S(1)} %fusion.129), channel_id=1, replica_groups=mesh['row'=8,'col'=4] {'row','col'}, use_global_device_ids=true, to_apply=%region_9.0 | all-reduce | flops 1641 | bytes 13128 | tf_op jit(solution)/shard_map/psum | solution.py:13
  297.4 1.5 fusion.75
  298.9 8.9 %all_gather.13 = bf16[16384]{0:T(1024)(128)(2,1)S(1)} all-gather(bf16[4096]{0:T(1024)(128)(2,1)S(1)} %get-tuple-element.31), channel_id=1, replica_groups=mesh['row'=8,'col'=4] {'col'}, dimensions={0}, use_global_device_ids=true | all-gather | bytes 40960 | tf_op jit(solution)/shard_map/all_gather | solution.py:84
  308.6 4.6 fusion.21
  314.4 53.6 %all-reduce.16.cloned.1.call-done = f32[16384]{0:T(1024)} async-done(((f32[16384]{0:T(1024)}), f32[16384]{0:T(1024)}) %all-reduce.16.cloned.1.call-update) | async-done | bytes 65552
  369.1 39.2 %psum.127 = f32[41]{0:T(128)S(1)} all-reduce(f32[41]{0:T(128)S(1)} %convolution_bitcast_fusion.16), channel_id=1, replica_groups=mesh['row'=8,'col'=4] {'row','col'}, use_global_device_ids=true, to_apply=%region_14.0 | all-reduce | flops 41 | bytes 328 | tf_op jit(solution)/shard_map/psum | solution.py:11
  410.3 40.0 %all-reduce.6 = (f32[41]{0:T(128)S(1)}, f32[]{:T(128)}) all-reduce(f32[41]{0:T(128)S(1)} %convolution_bitcast_fusion.15, f32[]{:T(128)} %get-tuple-element.29), channel_id=1, replica_groups=mesh['row'=8,'col'=4] {'row','col'}, use_global_device_ids=true, to_apply=%region_15.0 | all-reduce | flops 42 | bytes 336 | tf_op jit(solution)/shard_map/psum | solution.py:13
  453.5 14.1 %all_gather.14 = bf16[16384]{0:T(1024)(128)(2,1)S(1)} all-gather(bf16[2048]{0:T(1024)(128)(2,1)S(1)} %get-tuple-element.27), channel_id=1, replica_groups=mesh['row'=8,'col'=4] {'row'}, dimensions={0}, use_global_device_ids=true | all-gather | bytes 36864 | tf_op jit(solution)/shard_map/all_gather | solution.py:75
  468.4 5.6 fusion.18
  475.2 41.8 %all-reduce.18.cloned.1.call-done = f32[16384]{0:T(1024)} async-done(((f32[16384]{0:T(1024)}), f32[16384]{0:T(1024)}) %all-reduce.18.cloned.1.call-update) | async-done | bytes 65552
  518.4 39.2 %psum.130 = f32[41]{0:T(128)S(1)} all-reduce(f32[41]{0:T(128)S(1)} %convolution_bitcast_fusion.7), channel_id=1, replica_groups=mesh['row'=8,'col'=4] {'row','col'}, use_global_device_ids=true, to_apply=%region_19.0 | all-reduce | flops 41 | bytes 328 | tf_op jit(solution)/shard_map/psum | solution.py:11
  558.2 1.3 multiply_reduce_fusion
  560.2 41.4 %all-reduce.5 = (f32[41]{0:T(128)S(1)}, f32[]{:T(128)}) all-reduce(f32[41]{0:T(128)S(1)} %convolution_bitcast_fusion.6, f32[]{:T(128)} %get-tuple-element.25), channel_id=1, replica_groups=mesh['row'=8,'col'=4] {'row','col'}, use_global_device_ids=true, to_apply=%region_20.0 | all-reduce | flops 42 | bytes 336 | tf_op jit(solution)/shard_map/psum | solution.py:13
  605.6 9.1 %all_gather.15 = bf16[16384]{0:T(1024)(128)(2,1)S(1)} all-gather(bf16[4096]{0:T(1024)(128)(2,1)S(1)} %get-tuple-element.23), channel_id=1, replica_groups=mesh['row'=8,'col'=4] {'col'}, dimensions={0}, use_global_device_ids=true | all-gather | bytes 40960 | tf_op jit(solution)/shard_map/all_gather | solution.py:84
  615.4 4.6 fusion.15
  621.9 52.8 %all-reduce.20.cloned.1.call-done = f32[16384]{0:T(1024)} async-done(((f32[16384]{0:T(1024)}), f32[16384]{0:T(1024)}) %all-reduce.20.cloned.1.call-update) | async-done | bytes 65552
  675.8 39.3 %psum.133 = f32[42]{0:T(128)S(1)} all-reduce(f32[42]{0:T(128)S(1)} %convolution_bitcast_fusion.14), channel_id=1, replica_groups=mesh['row'=8,'col'=4] {'row','col'}, use_global_device_ids=true, to_apply=%region_24.0 | all-reduce | flops 42 | bytes 336 | tf_op jit(solution)/shard_map/psum | solution.py:11
  717.1 40.0 %all-reduce.4 = (f32[42]{0:T(128)S(1)}, f32[]{:T(128)}) all-reduce(f32[42]{0:T(128)S(1)} %convolution_bitcast_fusion.13, f32[]{:T(128)} %get-tuple-element.21), channel_id=1, replica_groups=mesh['row'=8,'col'=4] {'row','col'}, use_global_device_ids=true, to_apply=%region_25.0 | all-reduce | flops 43 | bytes 344 | tf_op jit(solution)/shard_map/psum | solution.py:13
  (104 shorter events, 34.0 us)
Async XLA Ops:
  7.2 5.3 copy-start
  7.2 10.6 %copy-start.7 = (u32[32]{0:T(128)S(1)}, u32[32]{0:T(128)}, u32[]{:S(2)}) copy-start(u32[32]{0:T(128)} %constant.69) | copy-start | bytes 388
  7.2 11.1 %copy-start.6 = (u32[32]{0:T(128)S(1)}, u32[32]{0:T(128)}, u32[]{:S(2)}) copy-start(u32[32]{0:T(128)} %constant.73) | copy-start | bytes 388
  7.2 13.0 %copy-start.5 = (s32[64]{0:T(128)S(1)}, s32[64]{0:T(128)}, u32[]{:S(2)}) copy-start(s32[64]{0:T(128)} %param.16) | copy-start | bytes 772
  7.2 13.1 %copy-start.4 = (s32[64]{0:T(128)S(1)}, s32[64]{0:T(128)}, u32[]{:S(2)}) copy-start(s32[64]{0:T(128)} %param.15) | copy-start | bytes 772
  7.2 46.0 %copy-start.3 = (f32[2048]{0:T(1024)S(1)}, f32[2048]{0:T(1024)}, u32[]{:S(2)}) copy-start(f32[2048]{0:T(1024)} %param.13) | copy-start | bytes 24580
  7.2 45.9 %reduce-scatter.5.cloned.1.call-start = ((), (), s32[]{:S(2)}) async-start(), calls=%async_computation.3 | async-start | bytes 2949120 | tf_op jit(solution)/shard_map/reduce_scatter | solution.py:46
  12.5 153.0 %reduce-scatter.3.cloned.1.call-start = ((), (), s32[]{:S(2)}) async-start(), calls=%async_computation.2 | async-start | bytes 3276800 | tf_op jit(solution)/shard_map/reduce_scatter | solution.py:41
  17.0 189.8 %all-reduce.14.cloned.1.call-start = ((), (), s32[]{:S(2)}) async-start(), calls=%async_computation.4 | async-start | bytes 131072
  165.4 202.6 %all-reduce.16.cloned.1.call-start = ((), (), s32[]{:S(2)}) async-start(), calls=%async_computation.5 | async-start | bytes 131072
  308.6 60.1 %copy-start.2 = (f32[40,2048]{1,0:T(8,128)S(1)}, f32[40,2048]{1,0:T(8,128)}, u32[]{:S(2)}) copy-start(f32[40,2048]{1,0:T(8,128)} %reduce-scatter.5.cloned.1.call-done) | copy-start | bytes 983044
  313.2 204.5 %copy-start.1 = (f32[40,4096]{1,0:T(8,128)S(1)}, f32[40,4096]{1,0:T(8,128)}, u32[]{:S(2)}) copy-start(f32[40,4096]{1,0:T(8,128)} %reduce-scatter.3.cloned.1.call-done) | copy-start | bytes 1966084
  314.1 202.9 %all-reduce.18.cloned.1.call-start = ((), (), s32[]{:S(2)}) async-start(), calls=%async_computation.6 | async-start | bytes 131072
  474.9 199.8 %all-reduce.20.cloned.1.call-start = ((), (), s32[]{:S(2)}) async-start(), calls=%async_computation.7 | async-start | bytes 131072
Sparse Core Ops, SparseCore 0:
  12.6 40.5 reduce-scatter.4
  56.2 39.4 reduce-scatter.2
  165.5 41.3 all-reduce.13
  314.2 53.6 all-reduce.15
  475.0 41.9 all-reduce.17
  621.0 53.6 all-reduce.19
where the time goes:
time: 772 us; the launch traced here: 769 us
  blocking collectives  447 us (58%)
  waiting for transfers between devices  221 us (29%)
  matrix products  55.3 us (7%)
  between operations  26.5 us (3%)
  other arithmetic  9.86 us (1%)
  local copies, waits for them, and re-layouts  9.85 us (1%)
    psum x5, blocking collectives, orthonormal(): lax.psum((jnp.dot(basis_rows, once_clean, precision=HIGH), jnp.sum(once_c...  205 us
    psum x5, blocking collectives, orthonormal(): lax.psum(jnp.dot(basis_rows, vector, precision=HIGH), ('row', 'col'))  196 us
    unnamed x10, waiting for transfers between devices  188 us
    reduce_scatter x1, waiting for transfers between devices, per_device(): lax.psum_scatter(jnp.dot(v_part.T, v_start, precision=HIGH), 'row', scatt...  32.9 us
    all_gather x2, blocking collectives, per_device(): lax.all_gather(current.astype(jnp.bfloat16), 'row', axis=0, tiled=True)  28.2 us
    all_gather x2, blocking collectives, per_device(): lax.all_gather(left_new.astype(jnp.bfloat16), 'col', axis=0, tiled=True)  18.1 us
  transfers between devices with their start and end apart: 6, of which 5 were waited for; matrix products, arithmetic and copies ran while one was open for 3% of the time, Pallas kernels for 0%

commit v1 on v0

--- a/solution.py
+++ b/solution.py
@@ -2,13 +2,18 @@
 import jax.numpy as jnp
 from jax import lax
 from jax.sharding import PartitionSpec as P
+from jax.lax import all_gather
 
 STEPS = 2
 HIGH = lax.Precision.HIGHEST
 
 
+def replace_shifts_all(here_x):
+    return all_gather(here_x, ("row", "col")).sum(axis=0)
+
+
 def orthonormal(basis_rows, vector, length, gram_matrix):
-    first_coef = lax.psum(jnp.dot(basis_rows, vector, precision=HIGH), ("row", "col")) / length
+    first_coef = replace_shifts_all(jnp.dot(basis_rows, vector, precision=HIGH)) / length
     once_clean = vector - jnp.dot(first_coef, basis_rows, precision=HIGH)
     second_coef, mean_square = lax.psum(
         (jnp.dot(basis_rows, once_clean, precision=HIGH), jnp.sum(once_clean * once_clean)),

time: 772 us -> 774 us (level)
    unnamed x0 -> x5, blocking collectives: none -> 196 us
    psum x5 -> x0, blocking collectives: 196 us -> none  [orthonormal(): lax.psum(jnp.dot(basis_rows, vector, precision=HIGH), ('row', 'col'))]
where the time goes in v1:
time: 774 us; the launch traced here: 771 us
  blocking collectives  447 us (58%)
  waiting for transfers between devices  221 us (29%)
  matrix products  55.3 us (7%)
  between operations  26.5 us (3%)
  local copies, waits for them, and re-layouts  11.4 us (1%)
  other arithmetic  9.98 us (1%)
    psum x5, blocking collectives, orthonormal(): lax.psum((jnp.dot(basis_rows, once_clean, precision=HIGH), jnp.sum(once_c...  205 us
    unnamed x5, blocking collectives  196 us
    unnamed x10, waiting for transfers between devices  188 us
    reduce_scatter x1, waiting for transfers between devices, per_device(): lax.psum_scatter(jnp.dot(v_part.T, v_start, precision=HIGH), 'row', scatt...  32.9 us
    all_gather x2, blocking collectives, per_device(): lax.all_gather(current.astype(jnp.bfloat16), 'row', axis=0, tiled=True)  28.2 us
    all_gather x2, blocking collectives, per_device(): lax.all_gather(left_new.astype(jnp.bfloat16), 'col', axis=0, tiled=True)  18.1 us
  transfers between devices with their start and end apart: 6, of which 5 were waited for; matrix products, arithmetic and copies ran while one was open for 3% of the time, Pallas kernels for 0%

profile of v1, /device:TPU:0, one launch (start us, length us, event | category | flops | bytes accessed | tf_op | source)
XLA Modules:
  0.0 771.5 jit_solution(1003190782267350119)
XLA Ops:
  7.3 5.1 fusion.49
  12.5 4.5 fusion.51
  20.3 32.9 %reduce-scatter.5.cloned.1.call-done = f32[40,2048]{1,0:T(8,128)} async-done(((f32[40,16384]{1,0:T(8,128)}), f32[40,2048]{1,0:T(8,128)}) %reduce-scatter.5.cloned.1.call-update) | async-done | bytes 327696 | tf_op jit(solution)/shard_map/reduce_scatter | solution.py:51
  54.7 38.3 %all-reduce = f32[1280]{0:T(1024)S(1)} all-reduce(f32[1280]{0:T(1024)S(1)} %dynamic-update-slice), channel_id=2, replica_groups=mesh['row'=8,'col'=4] {'row','col'}, use_global_device_ids=true, to_apply=%add | all-reduce | flops 1280 | bytes 10240
  96.3 1.6 fusion.128
  97.9 42.2 %all-reduce.13 = (f32[40]{0:T(128)S(1)}, f32[]{:T(128)}, f32[40,40]{1,0:T(8,128)S(1)}) all-reduce(f32[40]{0:T(128)S(1)} %convolution_bitcast_fusion.17, f32[]{:T(128)} %get-tuple-element.37, f32[40,40]{1,0:T(8,128)S(1)} %fusion.128), channel_id=1, replica_groups=mesh['row'=8,'col'=4] {'row','col'}, use_global_device_ids=true, to_apply=%region_3.0 | all-reduce | flops 1641 | bytes 13128 | tf_op jit(solution)/shard_map/psum | solution.py:18
  144.1 14.1 %all_gather.44 = bf16[16384]{0:T(1024)(128)(2,1)S(1)} all-gather(bf16[2048]{0:T(1024)(128)(2,1)S(1)} %get-tuple-element.35), channel_id=1, replica_groups=mesh['row'=8,'col'=4] {'row'}, dimensions={0}, use_global_device_ids=true | all-gather | bytes 36864 | tf_op jit(solution)/shard_map/all_gather | solution.py:80
  158.9 5.6 fusion.24
  165.7 1.9 fusion.129
  167.7 39.6 %all-reduce.19.cloned.1.call-done = f32[16384]{0:T(1024)} async-done(((f32[16384]{0:T(1024)}), f32[16384]{0:T(1024)}) %all-reduce.19.cloned.1.call-update) | async-done | bytes 65552
  208.0 1.7 convolution_bitcast_fusion.11
  209.9 39.5 %all-reduce.1 = f32[1280]{0:T(1024)S(1)} all-reduce(f32[1280]{0:T(1024)S(1)} %dynamic-update-slice.1), channel_id=3, replica_groups=mesh['row'=8,'col'=4] {'row','col'}, use_global_device_ids=true, to_apply=%add.1 | all-reduce | flops 1280 | bytes 10240
  249.6 1.5 fusion.77
  252.4 1.7 convolution_bitcast_fusion.10
  254.1 41.4 %all-reduce.12 = (f32[40]{0:T(128)S(1)}, f32[]{:T(128)}, f32[40,40]{1,0:T(8,128)S(1)}) all-reduce(f32[40]{0:T(128)S(1)} %convolution_bitcast_fusion.10, f32[]{:T(128)} %get-tuple-element.33, f32[40,40]{1,0:T(8,128)S(1)} %fusion.129), channel_id=1, replica_groups=mesh['row'=8,'col'=4] {'row','col'}, use_global_device_ids=true, to_apply=%region_9.0 | all-reduce | flops 1641 | bytes 13128 | tf_op jit(solution)/shard_map/psum | solution.py:18
  298.3 1.5 fusion.75
  299.8 8.9 %all_gather.47 = bf16[16384]{0:T(1024)(128)(2,1)S(1)} all-gather(bf16[4096]{0:T(1024)(128)(2,1)S(1)} %get-tuple-element.31), channel_id=1, replica_groups=mesh['row'=8,'col'=4] {'col'}, dimensions={0}, use_global_device_ids=true | all-gather | bytes 40960 | tf_op jit(solution)/shard_map/all_gather | solution.py:89
  309.5 4.6 fusion.21
  315.3 53.6 %all-reduce.21.cloned.1.call-done = f32[16384]{0:T(1024)} async-done(((f32[16384]{0:T(1024)}), f32[16384]{0:T(1024)}) %all-reduce.21.cloned.1.call-update) | async-done | bytes 65552
  370.2 39.3 %all-reduce.2 = f32[1312]{0:T(1024)S(1)} all-reduce(f32[1312]{0:T(1024)S(1)} %dynamic-update-slice.2), channel_id=4, replica_groups=mesh['row'=8,'col'=4] {'row','col'}, use_global_device_ids=true, to_apply=%add.2 | all-reduce | flops 1312 | bytes 10496
  411.7 40.0 %all-reduce.11 = (f32[41]{0:T(128)S(1)}, f32[]{:T(128)}) all-reduce(f32[41]{0:T(128)S(1)} %convolution_bitcast_fusion.15, f32[]{:T(128)} %get-tuple-element.29), channel_id=1, replica_groups=mesh['row'=8,'col'=4] {'row','col'}, use_global_device_ids=true, to_apply=%region_15.0 | all-reduce | flops 42 | bytes 336 | tf_op jit(solution)/shard_map/psum | solution.py:18
  454.9 14.1 %all_gather.50 = bf16[16384]{0:T(1024)(128)(2,1)S(1)} all-gather(bf16[2048]{0:T(1024)(128)(2,1)S(1)} %get-tuple-element.27), channel_id=1, replica_groups=mesh['row'=8,'col'=4] {'row'}, dimensions={0}, use_global_device_ids=true | all-gather | bytes 36864 | tf_op jit(solution)/shard_map/all_gather | solution.py:80
  469.7 5.6 fusion.18
  476.5 41.8 %all-reduce.23.cloned.1.call-done = f32[16384]{0:T(1024)} async-done(((f32[16384]{0:T(1024)}), f32[16384]{0:T(1024)}) %all-reduce.23.cloned.1.call-update) | async-done | bytes 65552
  520.0 39.6 %all-reduce.3 = f32[1312]{0:T(1024)S(1)} all-reduce(f32[1312]{0:T(1024)S(1)} %dynamic-update-slice.3), channel_id=5, replica_groups=mesh['row'=8,'col'=4] {'row','col'}, use_global_device_ids=true, to_apply=%add.3 | all-reduce | flops 1312 | bytes 10496
  560.2 1.3 multiply_reduce_fusion
  562.2 41.2 %all-reduce.10 = (f32[41]{0:T(128)S(1)}, f32[]{:T(128)}) all-reduce(f32[41]{0:T(128)S(1)} %convolution_bitcast_fusion.6, f32[]{:T(128)} %get-tuple-element.25), channel_id=1, replica_groups=mesh['row'=8,'col'=4] {'row','col'}, use_global_device_ids=true, to_apply=%region_20.0 | all-reduce | flops 42 | bytes 336 | tf_op jit(solution)/shard_map/psum | solution.py:18
  607.3 9.1 %all_gather.53 = bf16[16384]{0:T(1024)(128)(2,1)S(1)} all-gather(bf16[4096]{0:T(1024)(128)(2,1)S(1)} %get-tuple-element.23), channel_id=1, replica_groups=mesh['row'=8,'col'=4] {'col'}, dimensions={0}, use_global_device_ids=true | all-gather | bytes 40960 | tf_op jit(solution)/shard_map/all_gather | solution.py:89
  617.2 4.6 fusion.15
  623.7 52.9 %all-reduce.25.cloned.1.call-done = f32[16384]{0:T(1024)} async-done(((f32[16384]{0:T(1024)}), f32[16384]{0:T(1024)}) %all-reduce.25.cloned.1.call-update) | async-done | bytes 65552
  677.9 39.3 %all-reduce.4 = f32[1344]{0:T(1024)S(1)} all-reduce(f32[1344]{0:T(1024)S(1)} %dynamic-update-slice.4), channel_id=6, replica_groups=mesh['row'=8,'col'=4] {'row','col'}, use_global_device_ids=true, to_apply=%add.4 | all-reduce | flops 1344 | bytes 10752
  719.4 40.0 %all-reduce.9 = (f32[42]{0:T(128)S(1)}, f32[]{:T(128)}) all-reduce(f32[42]{0:T(128)S(1)} %convolution_bitcast_fusion.13, f32[]{:T(128)} %get-tuple-element.21), channel_id=1, replica_groups=mesh['row'=8,'col'=4] {'row','col'}, use_global_device_ids=true, to_apply=%region_25.0 | all-reduce | flops 43 | bytes 344 | tf_op jit(solution)/shard_map/psum | solution.py:18
  (124 shorter events, 35.6 us)
Async XLA Ops:
  7.2 5.3 copy-start
  7.2 10.6 %copy-start.7 = (u32[32]{0:T(128)S(1)}, u32[32]{0:T(128)}, u32[]{:S(2)}) copy-start(u32[32]{0:T(128)} %constant.89) | copy-start | bytes 388
  7.2 11.1 %copy-start.6 = (u32[32]{0:T(128)S(1)}, u32[32]{0:T(128)}, u32[]{:S(2)}) copy-start(u32[32]{0:T(128)} %constant.93) | copy-start | bytes 388
  7.2 13.0 %copy-start.5 = (s32[64]{0:T(128)S(1)}, s32[64]{0:T(128)}, u32[]{:S(2)}) copy-start(s32[64]{0:T(128)} %param.16) | copy-start | bytes 772
  7.2 13.1 %copy-start.4 = (s32[64]{0:T(128)S(1)}, s32[64]{0:T(128)}, u32[]{:S(2)}) copy-start(s32[64]{0:T(128)} %param.15) | copy-start | bytes 772
  7.2 46.0 %copy-start.3 = (f32[2048]{0:T(1024)S(1)}, f32[2048]{0:T(1024)}, u32[]{:S(2)}) copy-start(f32[2048]{0:T(1024)} %param.13) | copy-start | bytes 24580
  7.2 45.9 %reduce-scatter.5.cloned.1.call-start = ((), (), s32[]{:S(2)}) async-start(), calls=%async_computation.3 | async-start | bytes 2949120 | tf_op jit(solution)/shard_map/reduce_scatter | solution.py:51
  12.5 153.2 %reduce-scatter.3.cloned.1.call-start = ((), (), s32[]{:S(2)}) async-start(), calls=%async_computation.2 | async-start | bytes 3276800 | tf_op jit(solution)/shard_map/reduce_scatter | solution.py:46
  17.0 190.3 %all-reduce.19.cloned.1.call-start = ((), (), s32[]{:S(2)}) async-start(), calls=%async_computation.4 | async-start | bytes 131072
  165.6 203.2 %all-reduce.21.cloned.1.call-start = ((), (), s32[]{:S(2)}) async-start(), calls=%async_computation.5 | async-start | bytes 131072
  309.5 60.1 %copy-start.2 = (f32[40,2048]{1,0:T(8,128)S(1)}, f32[40,2048]{1,0:T(8,128)}, u32[]{:S(2)}) copy-start(f32[40,2048]{1,0:T(8,128)} %reduce-scatter.5.cloned.1.call-done) | copy-start | bytes 983044
  314.1 204.9 %copy-start.1 = (f32[40,4096]{1,0:T(8,128)S(1)}, f32[40,4096]{1,0:T(8,128)}, u32[]{:S(2)}) copy-start(f32[40,4096]{1,0:T(8,128)} %reduce-scatter.3.cloned.1.call-done) | copy-start | bytes 1966084
  315.0 203.3 %all-reduce.23.cloned.1.call-start = ((), (), s32[]{:S(2)}) async-start(), calls=%async_computation.6 | async-start | bytes 131072
  476.2 200.3 %all-reduce.25.cloned.1.call-start = ((), (), s32[]{:S(2)}) async-start(), calls=%async_computation.7 | async-start | bytes 131072
Sparse Core Ops, SparseCore 0:
  12.6 40.5 reduce-scatter.4
  56.2 39.3 reduce-scatter.2
  165.7 41.5 all-reduce.18
  315.1 53.6 all-reduce.20
  476.4 41.9 all-reduce.22
  622.8 53.7 all-reduce.24
